TPU v7x, 32 devices: a whole 2x2x4 slice. The times are simulated.
32 devices in a mesh: groups: 2 (over y), row: 16 (over z, x, core).
Axes of the slice: x: 2, y: 2, z: 4, core: 2. Of those that a mesh axis runs over, the one named last changes fastest.
Arguments:
- walkers: bfloat16 [64, 1024, 256], P('groups', 'row'), parts along dimension 0, may hold values from -6 to 6
- cholesky: bfloat16 [1024, 1024, 1024], P('groups', 'row'), parts along dimension 0, may hold values from -0.03125 to 0.03125
- slab_index: int32 [4, 64], P('groups'), parts along dimension 0, may hold values from 0 to 511
- fields: bfloat16 [2, 64, 64], P(None, ('groups', 'row')), parts along dimension 1, may hold values from -5 to 5
- counts: int32 [32], P('groups'), parts along dimension 0, may hold values from 1 to 2, as said below
- sources: int32 [4, 32], P('groups'), parts along dimension 0, may hold values from 0 to 31, as said below
Outputs:
- branched: bfloat16 [64, 1024, 256], P('groups', 'row'), parts along dimension 0
There are 2 independent parts, one for each index of `groups`. A program takes and returns all parts, laid end to end along the dimension named above; each array names one. Nothing has to cross between parts.
Inputs may be any that keep to these rules, and one draw needn't show every extreme that they name: counts[d] walkers live in the first counts[d] of the 2 slots d * 2 ... ; some index has all 2 live. For a living slot j, sources[s, j] is a living slot; for any other slot it is j itself.
All inputs are finite; a program needn't handle non-finite values.
Results may differ from a plain program's by a relative error of at most 0.0086.
Values may be sent and summed in bfloat16 or wider, within the bound.
A program may use at most 192 MiB of HBM per device.

v0:
```python
import jax
import jax.numpy as jnp
from jax import lax
from jax.sharding import PartitionSpec as P

SLAB = 64
STEPS = 2


def taylor_step(potential, initial):
    summed = initial.astype(jnp.float32)
    term_now = initial
    for degree in range(1, 5):
        product = jnp.dot(potential, term_now, preferred_element_type=jnp.float32) / degree
        summed = summed + product
        term_now = product.astype(jnp.bfloat16)
    return summed.astype(jnp.bfloat16)


def on_device(walkers, cholesky, slab_index, fields, counts, sources):
    local_rows = walkers.shape[1]
    orbitals = cholesky.shape[2]
    per_device = fields.shape[1]
    row_devices = lax.axis_size("row")
    slot_count = per_device * row_devices
    my_index = lax.axis_index("row")
    all_fields = lax.all_gather(fields, "row", axis=1, tiled=True)
    slot_ids = jnp.arange(slot_count, dtype=jnp.int32)
    owners = slot_ids // per_device
    within = slot_ids % per_device
    owner_counts = jnp.take(counts, owners)
    living = within < owner_counts
    before = jnp.cumsum(counts) - counts
    live_total = jnp.sum(counts)
    owner_before = jnp.take(before, owners)
    ordinal = jnp.where(
        living,
        owner_before + within,
        live_total + owners * per_device - owner_before + within - owner_counts,
    )
    position = ordinal % row_devices * per_device + ordinal // row_devices
    placed = jnp.zeros((slot_count,), jnp.int32).at[position].set(slot_ids)
    busy_slots = (live_total - my_index + row_devices - 1) // row_devices
    current = walkers
    for step_number in range(STEPS):
        chosen = jnp.take(cholesky, slab_index[step_number], axis=0).reshape(
            SLAB, local_rows * orbitals
        )
        ordered_fields = jnp.take(all_fields[step_number], placed, axis=0)
        potential_rows = (
            jnp.dot(ordered_fields, chosen, preferred_element_type=jnp.float32)
            .astype(jnp.bfloat16)
            .reshape(slot_count, local_rows, orbitals)
        )
        ordered = jnp.take(current, placed, axis=0)
        potentials, columns = (
            lax.all_to_all(potential_rows, "row", split_axis=0, concat_axis=1, tiled=True),
            lax.all_to_all(ordered, "row", split_axis=0, concat_axis=1, tiled=True),
        )

        def advance(walker, buffer):
            matrix = lax.dynamic_index_in_dim(potentials, walker, 0, keepdims=False)
            initial = lax.dynamic_index_in_dim(columns, walker, 0, keepdims=False)
            return lax.dynamic_update_index_in_dim(buffer, taylor_step(matrix, initial), walker, 0)

        advanced = lax.fori_loop(0, busy_slots, advance, jnp.zeros_like(columns))
        returned = lax.all_to_all(advanced, "row", split_axis=1, concat_axis=0, tiled=True)
        current = jnp.take(returned, jnp.take(position, sources[step_number]), axis=0)
    return current


def solution(mesh):
    in_specs = (
        P("groups", "row", None),
        P("groups", "row", None),
        P("groups", None),
        P(None, ("groups", "row"), None),
        P("groups"),
        P("groups", None),
    )
    out_specs = P("groups", "row", None)
    return jax.shard_map(
        on_device, mesh=mesh, in_specs=in_specs, out_specs=out_specs, check_vma=False
    )
```

profile of v0, /device:TPU:9, one launch (start us, length us, event | category | flops | bytes accessed | tf_op | source)
XLA Modules:
  0.0 391.5 jit_solution(3536680181950253770)
XLA Ops:
  1.0 1.4 fusion.98
  2.3 1.4 gather_fusion
  6.4 1.1 broadcast_select_fusion.3
  7.6 6.5 %all-to-all-start = ((bf16[32,64,256]{2,1,0:T(8,128)(2,1)}), bf16[32,64,256]{2,1,0:T(8,128)(2,1)S(1)}, u32[]{:S(2)}, u32[]{:S(2)}) async-start(bf16[32,64,256]{2,1,0:T(8,128)(2,1)} %broadcast_select_fusion.3), calls=%async_computation | async-start | bytes 2097152 | tf_op jit(solution)/shard_map/all_to_all | solution.py:58
  14.2 7.6 %gather_fusion.4 = bf16[64,64,1024]{2,1,0:T(8,128)(2,1)} fusion(bf16[512,64,1024]{2,1,0:T(8,128)(2,1)} %param.21, s32[1024]{0:T(1024)S(1)} %pad_clamp_fusion.3), kind=kCustom, calls=%fused_computation.2.clone | custom fusion | bytes 16777472 | tf_op jit(solution)/shard_map/jit(_take)/gather | solution.py:46
  21.8 7.6 %gather_fusion.9 = bf16[64,64,1024]{2,1,0:T(8,128)(2,1)} fusion(bf16[512,64,1024]{2,1,0:T(8,128)(2,1)} %param.21, s32[1024]{0:T(1024)S(1)} %pad_clamp_fusion.1), kind=kCustom, calls=%fused_computation.7.clone | custom fusion | bytes 16777472 | tf_op jit(solution)/shard_map/jit(_take)/gather | solution.py:46
  29.3 11.8 %broadcast_select_fusion = (bf16[64,64,1024]{2,1,0:T(8,128)(2,1)}, bf16[64,64,1024]{2,1,0:T(8,128)(2,1)}) fusion(bf16[64,64,1024]{2,1,0:T(8,128)(2,1)} %gather_fusion.9, pred[64]{0:T(512)(128)(4,1)S(1)} %get-tuple-element.90, bf16[64,64,1024]{2,1,0:T(8,128)(2,1)} %gather_fusion.4, pred[64]{0:T(512)(128)(4,1)S(1)} %get-tuple-element.104), kind=kLoop, calls=%fused_computation.71 | loop fusion | flops 8388608 | bytes 33554560 | tf_op jit(solution)/shard_map/jit(_take)/select_n | solution.py:46
  41.1 11.9 %copy.38 = bf16[8,8,64,1024]{3,1,2,0:T(8,128)(2,1)} copy(bf16[8,8,64,1024]{3,2,1,0:T(8,128)(2,1)} %bitcast.149) | data formatting | bytes 16777216
  53.1 19.0 %all_gather.3 = bf16[2,32,64]{2,0,1:T(2,128)(2,1)S(1)} all-gather(bf16[2,2,64]{2,0,1:T(2,128)(2,1)S(1)} %copy.24), channel_id=1, replica_groups=mesh['groups'=2,'row'=16] {'row'}, dimensions={1}, use_global_device_ids=true | all-gather | bytes 8704 | tf_op jit(solution)/shard_map/all_gather | solution.py:27
  72.7 4.7 %convolution_convert_fusion.1 = bf16[32,65536]{1,0:T(8,128)(2,1)S(1)} fusion(bf16[64,65536]{1,0:T(8,128)(2,1)} %bitcast.150, bf16[32,64]{1,0:T(8,128)(2,1)S(1)} %gather_fusion.3, pred[32]{0:T(512)(128)(4,1)S(1)} %compare_and_fusion.2), kind=kOutput, calls=%fused_computation.70 | convolution fusion | flops 270534656 | bytes 12587040 | tf_op jit(solution)/shard_map/dot_general | solution.py:51
  77.4 4.3 %copy.39 = bf16[4,8,64,1024]{3,2,1,0:T(8,128)(2,1)} copy(bf16[4,8,64,1024]{3,1,2,0:T(8,128)(2,1)S(1)} %bitcast.154) | data formatting | bytes 8388608
  81.6 7.3 %all-to-all-start.1 = ((bf16[32,64,1024]{2,1,0:T(8,128)(2,1)}), bf16[32,64,1024]{2,1,0:T(8,128)(2,1)}, u32[]{:S(2)}, u32[]{:S(2)}) async-start(bf16[32,64,1024]{2,1,0:T(8,128)(2,1)} %bitcast.152), calls=%async_computation.1 | async-start | bytes 8388608 | tf_op jit(solution)/shard_map/all_to_all | solution.py:57
  89.7 89.5 %all-to-all-done.1 = bf16[32,64,1024]{2,1,0:T(8,128)(2,1)} async-done(((bf16[32,64,1024]{2,1,0:T(8,128)(2,1)}), bf16[32,64,1024]{2,1,0:T(8,128)(2,1)}, u32[]{:S(2)}, u32[]{:S(2)}) %all-to-all-start.1) | async-done | bytes 4194336 | tf_op jit(solution)/shard_map/all_to_all | solution.py:57
  179.2 4.8 %copy.26 = bf16[16,2,64,1024]{3,2,0,1:T(8,128)(2,1)} copy(bf16[16,2,64,1024]{3,2,1,0:T(8,128)(2,1)} %bitcast.14) | data formatting | bytes 8388608 | tf_op jit(solution)/shard_map/all_to_all | solution.py:57
  184.1 5.1 %while.20 = (s32[]{:T(128)}, bf16[2,1024,256]{2,1,0:T(8,128)(2,1)S(1)}, s32[]{:T(128)}, bf16[2,1024,256]{2,1,0:T(8,128)(2,1)S(1)}, bf16[2,1024,1024]{2,1,0:T(8,128)(2,1)}, /*index=5*/s32[]{:T(128)}, s32[]{:T(128)}, s32[]{:T(128)}) while((s32[]{:T(128)}, bf16[2,1024,256]{2,1,0:T(8,128)(2,1)S(1)}, s32[]{:T(128)}, ...), condition=%wide.region_4.9_spmd, body=%wide.region_3.8_spmd.sunk | while | flops 2150629376 | bytes 36178072 | solution.py:66
  184.1 2.5 fusion.133
  189.2 2.0 copy.27
  191.3 7.0 %all-to-all-start.2 = ((bf16[2,1024,256]{2,0,1:T(2,128)(2,1)}), bf16[2,1024,256]{2,0,1:T(2,128)(2,1)S(1)}, u32[]{:S(2)}, u32[]{:S(2)}) async-start(bf16[2,1024,256]{2,0,1:T(2,128)(2,1)} %copy.27), calls=%async_computation.2 | async-start | bytes 2097152 | tf_op jit(solution)/shard_map/all_to_all | solution.py:67
  198.3 11.9 %copy.40 = bf16[8,8,64,1024]{3,1,2,0:T(8,128)(2,1)} copy(bf16[8,8,64,1024]{3,2,1,0:T(8,128)(2,1)} %bitcast.148) | data formatting | bytes 16777216
  210.8 4.7 %convolution_convert_fusion = bf16[32,65536]{1,0:T(8,128)(2,1)S(1)} fusion(bf16[64,65536]{1,0:T(8,128)(2,1)} %bitcast.151, bf16[32,64]{1,0:T(8,128)(2,1)S(1)} %gather_fusion.8, pred[32]{0:T(512)(128)(4,1)S(1)} %compare_and_fusion.2), kind=kOutput, calls=%fused_computation.69 | convolution fusion | flops 270534656 | bytes 12587040 | tf_op jit(solution)/shard_map/dot_general | solution.py:51
  215.5 4.3 %copy.41 = bf16[4,8,64,1024]{3,2,1,0:T(8,128)(2,1)} copy(bf16[4,8,64,1024]{3,1,2,0:T(8,128)(2,1)S(1)} %bitcast.155) | data formatting | bytes 8388608
  219.8 3.4 all-to-all-done.2
  223.2 4.9 %all-to-all-start.4 = ((bf16[32,64,1024]{2,1,0:T(8,128)(2,1)}), bf16[32,64,1024]{2,1,0:T(8,128)(2,1)}, u32[]{:S(2)}, u32[]{:S(2)}) async-start(bf16[32,64,1024]{2,1,0:T(8,128)(2,1)} %bitcast.153), calls=%async_computation.4 | async-start | bytes 8388608 | tf_op jit(solution)/shard_map/all_to_all | solution.py:57
  232.4 85.9 %all-to-all-done.4 = bf16[32,64,1024]{2,1,0:T(8,128)(2,1)} async-done(((bf16[32,64,1024]{2,1,0:T(8,128)(2,1)}), bf16[32,64,1024]{2,1,0:T(8,128)(2,1)}, u32[]{:S(2)}, u32[]{:S(2)}) %all-to-all-start.4) | async-done | bytes 4194336 | tf_op jit(solution)/shard_map/all_to_all | solution.py:57
  318.3 7.0 %all-to-all-start.3 = ((bf16[32,64,256]{2,1,0:T(8,128)(2,1)}), bf16[32,64,256]{2,1,0:T(8,128)(2,1)S(1)}, u32[]{:S(2)}, u32[]{:S(2)}) async-start(bf16[32,64,256]{2,1,0:T(8,128)(2,1)} %broadcast_select_fusion.4), calls=%async_computation.3 | async-start | bytes 2097152 | tf_op jit(solution)/shard_map/all_to_all | solution.py:58
  325.4 4.9 %copy.32 = bf16[16,2,64,1024]{3,2,0,1:T(8,128)(2,1)} copy(bf16[16,2,64,1024]{3,2,1,0:T(8,128)(2,1)} %bitcast.25) | data formatting | bytes 8388608 | tf_op jit(solution)/shard_map/all_to_all | solution.py:57
  330.2 20.1 %all-to-all-done.3 = bf16[32,64,256]{2,1,0:T(8,128)(2,1)S(1)} async-done(((bf16[32,64,256]{2,1,0:T(8,128)(2,1)}), bf16[32,64,256]{2,1,0:T(8,128)(2,1)S(1)}, u32[]{:S(2)}, u32[]{:S(2)}) %all-to-all-start.3) | async-done | bytes 1048608 | tf_op jit(solution)/shard_map/all_to_all | solution.py:58
  350.4 5.4 %while.21 = (s32[]{:T(128)}, bf16[2,1024,256]{2,1,0:T(8,128)(2,1)S(1)}, s32[]{:T(128)}, bf16[2,1024,256]{2,1,0:T(8,128)(2,1)S(1)}, bf16[2,1024,1024]{2,1,0:T(8,128)(2,1)}, /*index=5*/s32[]{:T(128)}, s32[]{:T(128)}, s32[]{:T(128)}) while((s32[]{:T(128)}, bf16[2,1024,256]{2,1,0:T(8,128)(2,1)S(1)}, s32[]{:T(128)}, ...), condition=%wide.region_6.12_spmd, body=%wide.region_5.11_spmd.sunk | while | flops 2150629376 | bytes 36178072 | solution.py:66
  350.7 2.5 fusion.145
  355.8 2.0 copy.33
  357.9 6.6 %all-to-all-start.5 = ((bf16[2,1024,256]{2,0,1:T(2,128)(2,1)}), bf16[2,1024,256]{2,0,1:T(2,128)(2,1)S(1)}, u32[]{:S(2)}, u32[]{:S(2)}) async-start(bf16[2,1024,256]{2,0,1:T(2,128)(2,1)} %copy.33), calls=%async_computation.5 | async-start | bytes 2097152 | tf_op jit(solution)/shard_map/all_to_all | solution.py:67
  364.5 24.9 %all-to-all-done.5 = bf16[2,1024,256]{2,0,1:T(2,128)(2,1)S(1)} async-done(((bf16[2,1024,256]{2,0,1:T(2,128)(2,1)}), bf16[2,1024,256]{2,0,1:T(2,128)(2,1)S(1)}, u32[]{:S(2)}, u32[]{:S(2)}) %all-to-all-start.5) | async-done | bytes 1048608 | tf_op jit(solution)/shard_map/all_to_all | solution.py:67
  (63 shorter events, 16.6 us)
Async XLA Ops:
  0.0 5.8 %copy-start = (bf16[32,64,256]{2,1,0:T(8,128)(2,1)S(1)}, bf16[32,64,256]{2,1,0:T(8,128)(2,1)}, u32[]{:S(2)}) copy-start(bf16[32,64,256]{2,1,0:T(8,128)(2,1)} %param.20) | copy-start | bytes 3145732
  0.0 14.1 %copy-start.5 = (s32[2,64]{1,0:T(2,128)S(1)}, s32[2,64]{1,0:T(2,128)}, u32[]{:S(2)}) copy-start(s32[2,64]{1,0:T(2,128)} %param.22) | copy-start | bytes 1540
  7.6 74.1 %all-to-all-start = ((bf16[32,64,256]{2,1,0:T(8,128)(2,1)}), bf16[32,64,256]{2,1,0:T(8,128)(2,1)S(1)}, u32[]{:S(2)}, u32[]{:S(2)}) async-start(bf16[32,64,256]{2,1,0:T(8,128)(2,1)} %broadcast_select_fusion.3), calls=%async_computation | async-start | bytes 2097152 | tf_op jit(solution)/shard_map/all_to_all | solution.py:58
  41.1 11.9 %copy-start.6 = (bf16[2,2,64]{2,1,0:T(2,128)(2,1)S(1)}, bf16[2,2,64]{2,1,0:T(2,128)(2,1)}, u32[]{:S(2)}) copy-start(bf16[2,2,64]{2,1,0:T(2,128)(2,1)} %param.23) | copy-start | bytes 1540
  81.6 97.6 %all-to-all-start.1 = ((bf16[32,64,1024]{2,1,0:T(8,128)(2,1)}), bf16[32,64,1024]{2,1,0:T(8,128)(2,1)}, u32[]{:S(2)}, u32[]{:S(2)}) async-start(bf16[32,64,1024]{2,1,0:T(8,128)(2,1)} %bitcast.152), calls=%async_computation.1 | async-start | bytes 8388608 | tf_op jit(solution)/shard_map/all_to_all | solution.py:57
  184.1 2.8 copy-start.3
  191.3 32.0 %all-to-all-start.2 = ((bf16[2,1024,256]{2,0,1:T(2,128)(2,1)}), bf16[2,1024,256]{2,0,1:T(2,128)(2,1)S(1)}, u32[]{:S(2)}, u32[]{:S(2)}) async-start(bf16[2,1024,256]{2,0,1:T(2,128)(2,1)} %copy.27), calls=%async_computation.2 | async-start | bytes 2097152 | tf_op jit(solution)/shard_map/all_to_all | solution.py:67
  223.2 4.9 %copy-start.4 = (s32[2,32]{1,0:T(2,128)S(1)}, s32[2,32]{1,0:T(2,128)}, u32[]{:S(2)}) copy-start(s32[2,32]{1,0:T(2,128)} %param.25) | copy-start | bytes 772
  223.2 95.1 %all-to-all-start.4 = ((bf16[32,64,1024]{2,1,0:T(8,128)(2,1)}), bf16[32,64,1024]{2,1,0:T(8,128)(2,1)}, u32[]{:S(2)}, u32[]{:S(2)}) async-start(bf16[32,64,1024]{2,1,0:T(8,128)(2,1)} %bitcast.153), calls=%async_computation.4 | async-start | bytes 8388608 | tf_op jit(solution)/shard_map/all_to_all | solution.py:57
  318.3 32.0 %all-to-all-start.3 = ((bf16[32,64,256]{2,1,0:T(8,128)(2,1)}), bf16[32,64,256]{2,1,0:T(8,128)(2,1)S(1)}, u32[]{:S(2)}, u32[]{:S(2)}) async-start(bf16[32,64,256]{2,1,0:T(8,128)(2,1)} %broadcast_select_fusion.4), calls=%async_computation.3 | async-start | bytes 2097152 | tf_op jit(solution)/shard_map/all_to_all | solution.py:58
  350.7 2.8 copy-start.2
  357.9 31.6 %all-to-all-start.5 = ((bf16[2,1024,256]{2,0,1:T(2,128)(2,1)}), bf16[2,1024,256]{2,0,1:T(2,128)(2,1)S(1)}, u32[]{:S(2)}, u32[]{:S(2)}) async-start(bf16[2,1024,256]{2,0,1:T(2,128)(2,1)} %copy.33), calls=%async_computation.5 | async-start | bytes 2097152 | tf_op jit(solution)/shard_map/all_to_all | solution.py:67
  364.5 27.0 %copy-start.1 = (bf16[32,64,256]{2,1,0:T(8,128)(2,1)S(1)}, bf16[32,64,256]{2,1,0:T(8,128)(2,1)}, u32[]{:S(2)}) copy-start(bf16[32,64,256]{2,1,0:T(8,128)(2,1)} %param.20) | copy-start | bytes 3145732
where the time goes:
time: 392 us; the launch traced here: 391 us
  waiting for transfers between devices  224 us (57%)
  local copies, waits for them, and re-layouts  71.5 us (18%)
  starting transfers between devices  39.5 us (10%)
  blocking collectives  19 us (5%)
  matrix products  18.8 us (5%)
  other arithmetic  17.6 us (4%)
    all_to_all x2, waiting for transfers between devices, on_device(): lax.all_to_all(potential_rows, 'row', split_axis=0, concat_axis=1, tiled=...  175 us
    unnamed x15, local copies, waits for them, and re-layouts  32.4 us
    all_to_all x2, waiting for transfers between devices, on_device(): lax.all_to_all(advanced, 'row', split_axis=1, concat_axis=0, tiled=True)  28.3 us
    all_to_all x2, waiting for transfers between devices, on_device(): lax.all_to_all(ordered, 'row', split_axis=0, concat_axis=1, tiled=True)  20.1 us
    all_gather x1, blocking collectives, on_device(): all_fields = lax.all_gather(fields, 'row', axis=1, tiled=True)  19 us
    gather x2, local copies, waits for them, and re-layouts, on_device(): jnp.take(cholesky, slab_index[step_number], axis=0)  15.2 us
    all_to_all x2, starting transfers between devices, on_device(): lax.all_to_all(advanced, 'row', split_axis=1, concat_axis=0, tiled=True)  13.7 us
    all_to_all x2, starting transfers between devices, on_device(): lax.all_to_all(ordered, 'row', split_axis=0, concat_axis=1, tiled=True)  13.6 us
  transfers between devices with their start and end apart: 6, of which 5 were waited for; matrix products, arithmetic and copies ran while one was open for 20% of the time, Pallas kernels for 0%

commit v1 on v0

--- a/solution.py
+++ b/solution.py
@@ -1,23 +1,29 @@
+import functools
+
 import jax
 import jax.numpy as jnp
 from jax import lax
+from jax.experimental import pallas as pl
+from jax.experimental.pallas import tpu as pltpu
 from jax.sharding import PartitionSpec as P
 
-SLAB = 64
-STEPS = 2
+MESH = pl.DeviceIdType.MESH
+ORDER = 4
+VMEM_BYTES = 60 * 1024 * 1024
 
 
 def taylor_step(potential, initial):
     summed = initial.astype(jnp.float32)
     term_now = initial
-    for degree in range(1, 5):
+    for degree in range(1, ORDER + 1):
         product = jnp.dot(potential, term_now, preferred_element_type=jnp.float32) / degree
         summed = summed + product
         term_now = product.astype(jnp.bfloat16)
     return summed.astype(jnp.bfloat16)
 
 
-def on_device(walkers, cholesky, slab_index, fields, counts, sources):
+def thin_rows(walkers, cholesky, slab_index, fields, counts, sources):
+    steps, slab = slab_index.shape
     local_rows = walkers.shape[1]
     orbitals = cholesky.shape[2]
     per_device = fields.shape[1]
@@ -42,9 +48,9 @@
     placed = jnp.zeros((slot_count,), jnp.int32).at[position].set(slot_ids)
     busy_slots = (live_total - my_index + row_devices - 1) // row_devices
     current = walkers
-    for step_number in range(STEPS):
+    for step_number in range(steps):
         chosen = jnp.take(cholesky, slab_index[step_number], axis=0).reshape(
-            SLAB, local_rows * orbitals
+            slab, local_rows * orbitals
         )
         ordered_fields = jnp.take(all_fields[step_number], placed, axis=0)
         potential_rows = (
@@ -67,6 +73,491 @@
         returned = lax.all_to_all(advanced, "row", split_axis=1, concat_axis=0, tiled=True)
         current = jnp.take(returned, jnp.take(position, sources[step_number]), axis=0)
     return current
+
+
+def enter(n, groups, me, group, across):
+    barrier = pltpu.get_barrier_semaphore()
+
+    def greet(k, carry):
+        pl.semaphore_signal(
+            barrier, inc=1, device_id={"row": lax.rem(me + k, n)}, device_id_type=MESH
+        )
+        return carry
+
+    lax.fori_loop(1, n, greet, 0)
+    others = 0
+    if across:
+        for k in range(1, groups):
+            others += 1
+            pl.semaphore_signal(
+                barrier,
+                inc=1,
+                device_id={"groups": lax.rem(group + k, groups)},
+                device_id_type=MESH,
+            )
+    pl.semaphore_wait(barrier, n - 1 + others)
+
+
+def gather_kernel(
+    n, groups, fields, counts, sources, all_fields, all_counts, all_sources,
+    landed, send, recv, far_send, far_recv,
+):
+    me, group = lax.axis_index("row"), lax.axis_index("groups")
+    enter(n, groups, me, group, True)
+
+    def copy(k, owner):
+        return pltpu.make_async_remote_copy(
+            src_ref=fields,
+            dst_ref=landed.at[owner],
+            send_sem=send.at[k],
+            recv_sem=recv.at[k],
+            device_id={"row": lax.rem(me + k, n)},
+            device_id_type=MESH,
+        )
+
+    def far(which, k, owner):
+        return pltpu.make_async_remote_copy(
+            src_ref=(counts, sources)[which],
+            dst_ref=(all_counts, all_sources)[which].at[owner],
+            send_sem=far_send.at[which, k],
+            recv_sem=far_recv.at[which, k],
+            device_id={"groups": lax.rem(group + k, groups)},
+            device_id_type=MESH,
+        )
+
+    def begin(k, carry):
+        copy(k, me).start()
+        return carry
+
+    def finish(k, carry):
+        copy(k, lax.rem(me - k + n, n)).wait()
+        return carry
+
+    lax.fori_loop(1, n, begin, 0)
+    for k in range(1, groups):
+        for which in range(2):
+            far(which, k, group).start()
+    landed[me] = fields[...]
+    all_counts[group] = counts[...]
+    all_sources[group] = sources[...]
+    lax.fori_loop(1, n, finish, 0)
+    for k in range(1, groups):
+        for which in range(2):
+            far(which, k, lax.rem(group - k + groups, groups)).wait()
+    all_fields[...] = landed[...].astype(jnp.float32)
+
+
+def gather_fields(n, groups, fields, counts, sources):
+    steps, per, slab = fields.shape
+    slots = n * per
+    vmem = pl.BlockSpec(memory_space=pltpu.VMEM)
+    return pl.pallas_call(
+        functools.partial(gather_kernel, n, groups),
+        out_shape=(
+            jax.ShapeDtypeStruct((n, steps, per, slab), jnp.float32),
+            jax.ShapeDtypeStruct((groups, 1, n), jnp.int32),
+            jax.ShapeDtypeStruct((groups, steps, slots), jnp.int32),
+        ),
+        in_specs=[vmem] * 3,
+        out_specs=(vmem,) * 3,
+        scratch_shapes=[
+            pltpu.VMEM((n, steps, per, slab), jnp.bfloat16),
+            pltpu.SemaphoreType.DMA((n,)),
+            pltpu.SemaphoreType.DMA((n,)),
+            pltpu.SemaphoreType.DMA((2, groups)),
+            pltpu.SemaphoreType.DMA((2, groups)),
+        ],
+        compiler_params=pltpu.CompilerParams(collective_id=0, has_side_effects=True),
+        name="gather_fields",
+    )(fields, counts.reshape(1, n), sources)
+
+
+def potential_kernel(
+    n, groups, per, block,
+    slab_index, counts, sources, fields, walkers, cholesky,
+    potential, ordered, parents, picks, fits,
+    chosen, made, left, spread, need, rank, slot, chol_sem, walk_sem, out_sem,
+):
+    steps, slab = slab_index.shape
+    slots = n * per
+    rows, orbitals = chosen.shape[2], chosen.shape[3]
+    group = lax.axis_index("groups")
+
+    def slab_copy(s, g):
+        return pltpu.make_async_copy(
+            cholesky.at[slab_index[s, g]], chosen.at[s, g], chol_sem.at[s, g]
+        )
+
+    for s in range(steps):
+        def fetch(g, carry):
+            slab_copy(s, g).start()
+            return carry
+
+        lax.fori_loop(0, slab, fetch, 0)
+
+    def plan(which):
+        def clear(j, carry):
+            for s in range(steps + 1):
+                need[s, j] = 0
+            for s in range(steps):
+                slot[s, j] = 0
+            return carry
+
+        def live(j, carry):
+            need[steps, j] = (lax.rem(j, per) < counts[which, 0, j // per]).astype(jnp.int32)
+            return carry
+
+        lax.fori_loop(0, slots, clear, 0)
+        lax.fori_loop(0, slots, live, 0)
+        total = 0
+        for s in reversed(range(steps)):
+            def mark(j, carry):
+                @pl.when(need[s + 1, j] == 1)
+                def _():
+                    need[s, sources[which, s, j]] = 1
+
+                return carry
+
+            def number(j, count):
+                rank[s, j] = count
+
+                @pl.when(need[s, j] == 1)
+                def _():
+                    slot[s, count] = j
+
+                return count + need[s, j]
+
+            lax.fori_loop(0, slots, mark, 0)
+            count = lax.fori_loop(0, slots, number, jnp.int32(0))
+            total = jnp.maximum(total, count)
+        return total
+
+    largest = jnp.int32(0)
+    for k in range(1, groups + 1):
+        own = plan(lax.rem(group + k, groups))
+        largest = jnp.maximum(largest, own)
+    fits[0] = (largest <= n).astype(jnp.int32)
+
+    def walker_copy(p):
+        return pltpu.make_async_copy(walkers.at[slot[0, p]], ordered.at[p], walk_sem.at[p])
+
+    def take_walker(p, carry):
+        walker_copy(p).start()
+        return carry
+
+    lax.fori_loop(0, slots, take_walker, 0)
+
+    def parent(p, carry):
+        for s in range(1, steps):
+            index = slot[s, p]
+            known = need[s, index]
+            parents[s - 1, p] = known * (1 + rank[s - 1, sources[group, s - 1, index]])
+        alive = need[steps, p]
+        picks[p] = alive * (1 + rank[steps - 1, sources[group, steps - 1, p]])
+        return carry
+
+    lax.fori_loop(0, slots, parent, 0)
+
+    wide = slab * block
+    column = lax.broadcasted_iota(jnp.int32, (slab, wide), 1)
+    owner = lax.broadcasted_iota(jnp.int32, (slab, wide), 0)
+    expand = jnp.where(column // block == owner, 1.0, 0.0).astype(jnp.bfloat16)
+
+    def out_copy(s, q):
+        return pltpu.make_async_copy(made.at[s], potential.at[s, pl.ds(q * n, n)], out_sem.at[s])
+
+    def build(s, q):
+        def field_row(p, carry):
+            index = slot[s, q * n + p]
+            line = fields[index // per, s, pl.ds(lax.rem(index, per), 1), :]
+            spread[pl.ds(pl.multiple_of(p * block, block), block), :] = jnp.broadcast_to(
+                line, (block, slab)
+            )
+            return carry
+
+        lax.fori_loop(0, n, field_row, 0)
+        across = jnp.dot(
+            spread[...].astype(jnp.bfloat16), expand, preferred_element_type=jnp.float32
+        )
+        row_in = lax.broadcasted_iota(jnp.int32, across.shape, 0) % block
+        column_in = lax.broadcasted_iota(jnp.int32, across.shape, 1) % block
+        left[...] = jnp.where(row_in == column_in, across, 0.0).astype(jnp.bfloat16)
+
+        def tile(b, carry):
+            lines = pl.ds(pl.multiple_of(b * block, block), block)
+            width = min(256, orbitals)
+            for c in range(0, orbitals, width):
+                right = chosen[s, :, lines, c : c + width].reshape(wide, width)
+                product = jnp.dot(left[...], right, preferred_element_type=jnp.float32)
+                made[s, :, lines, c : c + width] = product.astype(jnp.bfloat16).reshape(
+                    n, block, width
+                )
+            return carry
+
+        lax.fori_loop(0, rows // block, tile, 0)
+        out_copy(s, q).start()
+
+    for s in range(steps):
+        def arrive(g, carry):
+            slab_copy(s, g).wait()
+            return carry
+
+        lax.fori_loop(0, slab, arrive, 0)
+        build(s, 0)
+    for s in range(steps):
+        out_copy(s, 0).wait()
+
+    for q in range(1, per):
+        @pl.when(largest > n)
+        def _():
+            for s in range(steps):
+                build(s, q)
+            for s in range(steps):
+                out_copy(s, q).wait()
+
+    def walker_here(p, carry):
+        walker_copy(p).wait()
+        return carry
+
+    lax.fori_loop(0, slots, walker_here, 0)
+
+
+def make_potentials(n, groups, slab_index, counts, sources, fields, walkers, cholesky):
+    _, steps, per, slab = fields.shape
+    slots, rows, electrons = walkers.shape
+    orbitals = cholesky.shape[2]
+    block = 16
+    smem = pl.BlockSpec(memory_space=pltpu.SMEM)
+    vmem = pl.BlockSpec(memory_space=pltpu.VMEM)
+    anywhere = pl.BlockSpec(memory_space=pl.ANY)
+    return pl.pallas_call(
+        functools.partial(potential_kernel, n, groups, per, block),
+        out_shape=(
+            jax.ShapeDtypeStruct((steps, slots, rows, orbitals), jnp.bfloat16),
+            jax.ShapeDtypeStruct((slots, rows, electrons), jnp.bfloat16),
+            jax.ShapeDtypeStruct((max(steps - 1, 1), slots), jnp.int32),
+            jax.ShapeDtypeStruct((slots,), jnp.int32),
+            jax.ShapeDtypeStruct((1,), jnp.int32),
+        ),
+        in_specs=[smem, smem, smem, vmem, anywhere, anywhere],
+        out_specs=(anywhere, vmem, smem, smem, smem),
+        scratch_shapes=[
+            pltpu.VMEM((steps, slab, rows, orbitals), jnp.bfloat16),
+            pltpu.VMEM((steps, n, rows, orbitals), jnp.bfloat16),
+            pltpu.VMEM((n * block, slab * block), jnp.bfloat16),
+            pltpu.VMEM((n * block, slab), jnp.float32),
+            pltpu.SMEM((steps + 1, slots), jnp.int32),
+            pltpu.SMEM((steps, slots), jnp.int32),
+            pltpu.SMEM((steps, slots), jnp.int32),
+            pltpu.SemaphoreType.DMA((steps, slab)),
+            pltpu.SemaphoreType.DMA((slots,)),
+            pltpu.SemaphoreType.DMA((steps,)),
+        ],
+        compiler_params=pltpu.CompilerParams(vmem_limit_bytes=VMEM_BYTES),
+        name="make_potentials",
+    )(slab_index, counts, sources, fields, walkers, cholesky)
+
+
+def propagate_kernel(
+    n, per, potential, ordered, parents, picks, out,
+    matrices, columns, term, summed, advanced, turned, back0, back1,
+    v_send, v_recv, w_send, w_recv, r_send, r_recv, own_sem,
+):
+    steps = potential.shape[0]
+    rows, orbitals = potential.shape[2], potential.shape[3]
+    electrons = ordered.shape[2]
+    me = lax.axis_index("row")
+    back = (back0, back1)
+
+    def copy(source, target, sends, recvs, k):
+        return pltpu.make_async_remote_copy(
+            src_ref=source,
+            dst_ref=target,
+            send_sem=sends,
+            recv_sem=recvs,
+            device_id={"row": lax.rem(me + k, n)},
+            device_id_type=MESH,
+        )
+
+    def v_copy(s, q, k, owner):
+        return copy(
+            potential.at[s, q * n + lax.rem(me + k, n)],
+            matrices.at[s, q, owner],
+            v_send.at[s, q, k],
+            v_recv.at[s, q, k],
+            k,
+        )
+
+    def w_copy(s, q, k, owner):
+        source = ordered if s == 0 else turned
+        return copy(
+            source.at[q * n + lax.rem(me + k, n)],
+            columns.at[s, q, owner],
+            w_send.at[s, q, k],
+            w_recv.at[s, q, k],
+            k,
+        )
+
+    def r_copy(s, q, k, owner):
+        return copy(
+            advanced.at[s, q, lax.rem(me + k, n)],
+            back[s].at[1 + q * n + owner],
+            r_send.at[s, q, k],
+            r_recv.at[s, q, k],
+            k,
+        )
+
+    def own_v(s, q):
+        return pltpu.make_async_copy(
+            potential.at[s, q * n + me], matrices.at[s, q, me], own_sem.at[s, q]
+        )
+
+    def own_w(q):
+        return pltpu.make_async_copy(
+            ordered.at[q * n + me], columns.at[0, q, me], own_sem.at[steps, q]
+        )
+
+    def start(make, s, first=1, last=n):
+        def one(k, carry):
+            for q in range(per):
+                make(s, q, k, me).start()
+            return carry
+
+        lax.fori_loop(first, last, one, 0)
+
+    def received(make, s):
+        def one(k, carry):
+            for q in range(per):
+                make(s, q, k, lax.rem(me - k + n, n)).wait_recv()
+            return carry
+
+        lax.fori_loop(1, n, one, 0)
+
+    def sent(make, s):
+        def one(k, carry):
+            for q in range(per):
+                make(s, q, k, me).wait_send()
+            return carry
+
+        lax.fori_loop(1, n, one, 0)
+
+    def taylor(s, q):
+        term[0] = columns[s, q].reshape(n * rows, electrons)
+        summed[...] = columns[s, q].reshape(n * rows, electrons).astype(jnp.float32)
+        height = max(rows, min(256, n * rows))
+        count = height // rows
+
+        def degree(k, carry):
+            now, later = lax.rem(k - 1, 2), lax.rem(k, 2)
+            scale = jnp.where(k == 1, 1.0, jnp.where(k == 2, 0.5, jnp.where(k == 3, 1 / 3, 0.25)))
+            scale = scale.astype(jnp.float32)
+            for c in range(n // count):
+                matrix = matrices[s, q, c * count : (c + 1) * count].reshape(height, orbitals)
+                product = (
+                    jnp.dot(matrix, term[now], preferred_element_type=jnp.float32) * scale
+                )
+                lines = slice(c * height, (c + 1) * height)
+                summed[lines, :] = summed[lines, :] + product
+                term[later, lines, :] = product.astype(jnp.bfloat16)
+            return carry
+
+        lax.fori_loop(1, ORDER + 1, degree, 0)
+        advanced[s, q] = summed[...].astype(jnp.bfloat16).reshape(n, rows, electrons)
+
+    for s in range(steps):
+        back[s][0] = jnp.zeros((rows, electrons), jnp.bfloat16)
+    enter(n, 1, me, 0, False)
+    start(w_copy, 0)
+    start(v_copy, 0)
+    for q in range(per):
+        own_w(q).start()
+        for s in range(steps):
+            own_v(s, q).start()
+    for q in range(per):
+        own_w(q).wait()
+        for s in range(steps):
+            own_v(s, q).wait()
+    received(w_copy, 0)
+    received(v_copy, 0)
+    for s in range(steps):
+        if s + 1 < steps:
+            start(v_copy, s + 1, 1, n // 2)
+        for q in range(per):
+            taylor(s, q)
+        start(r_copy, s)
+        if s + 1 < steps:
+            start(v_copy, s + 1, n // 2, n)
+        for q in range(per):
+            back[s][1 + q * n + me] = advanced[s, q, me]
+        received(r_copy, s)
+        if s + 1 < steps:
+            def turn(p, carry):
+                turned[p] = back[s][parents[s, p]]
+                return carry
+
+            lax.fori_loop(0, n * per, turn, 0)
+            start(w_copy, s + 1)
+            for q in range(per):
+                columns[s + 1, q, me] = turned[q * n + me]
+            received(w_copy, s + 1)
+            received(v_copy, s + 1)
+
+    def pick(j, carry):
+        out[j] = back[steps - 1][picks[j]]
+        return carry
+
+    lax.fori_loop(0, out.shape[0], pick, 0)
+    for s in range(steps):
+        for make in (w_copy, v_copy, r_copy):
+            sent(make, s)
+
+
+def propagate(n, per, ident, potential, ordered, parents, picks):
+    steps, slots, rows, orbitals = potential.shape
+    electrons = ordered.shape[2]
+    smem = pl.BlockSpec(memory_space=pltpu.SMEM)
+    anywhere = pl.BlockSpec(memory_space=pl.ANY)
+    vmem = pl.BlockSpec(memory_space=pltpu.VMEM)
+    half = jnp.bfloat16
+    pairs = pltpu.SemaphoreType.DMA((steps, per, n))
+    return pl.pallas_call(
+        functools.partial(propagate_kernel, n, per),
+        out_shape=jax.ShapeDtypeStruct((slots, rows, electrons), half),
+        in_specs=[anywhere, anywhere, smem, smem],
+        out_specs=vmem,
+        scratch_shapes=[
+            pltpu.VMEM((steps, per, n, rows, orbitals), half),
+            pltpu.VMEM((steps, per, n, rows, electrons), half),
+            pltpu.VMEM((2, n * rows, electrons), half),
+            pltpu.VMEM((n * rows, electrons), jnp.float32),
+            pltpu.VMEM((steps, per, n, rows, electrons), half),
+            pltpu.VMEM((per * n, rows, electrons), half),
+            pltpu.VMEM((1 + per * n, rows, electrons), half),
+            pltpu.VMEM((1 + per * n, rows, electrons), half),
+            pairs, pairs, pairs, pairs, pairs, pairs,
+            pltpu.SemaphoreType.DMA((steps + 1, per)),
+        ],
+        compiler_params=pltpu.CompilerParams(
+            collective_id=ident, has_side_effects=True, vmem_limit_bytes=VMEM_BYTES
+        ),
+        name="propagate_%d" % per,
+    )(potential, ordered, parents, picks)
+
+
+def on_device(n, groups, walkers, cholesky, slab_index, fields, counts, sources):
+    if walkers.shape[1] % 16:
+        return thin_rows(walkers, cholesky, slab_index, fields, counts, sources)
+    per = fields.shape[1]
+    all_fields, all_counts, all_sources = gather_fields(n, groups, fields, counts, sources)
+    potential, ordered, parents, picks, fits = make_potentials(
+        n, groups, slab_index, all_counts, all_sources, all_fields, walkers, cholesky
+    )
+    return lax.cond(
+        fits[0] == 1,
+        lambda *args: propagate(n, 1, 1, *args),
+        lambda *args: propagate(n, per, 2, *args),
+        potential, ordered, parents, picks,
+    )
 
 
 def solution(mesh):
@@ -80,5 +571,6 @@
     )
     out_specs = P("groups", "row", None)
     return jax.shard_map(
-        on_device, mesh=mesh, in_specs=in_specs, out_specs=out_specs, check_vma=False
+        functools.partial(on_device, mesh.shape["row"], mesh.shape["groups"]),
+        mesh=mesh, in_specs=in_specs, out_specs=out_specs, check_vma=False,
     )

time: 392 us -> 190 us (0.48)
  waiting for transfers between devices: 224 us -> 0 us
  Pallas kernels: 0 us -> 188 us
  local copies, waits for them, and re-layouts: 71.5 us -> 0.97 us
  starting transfers between devices: 39.5 us -> 0 us
  blocking collectives: 19 us -> 0 us
  matrix products: 18.8 us -> 0 us
  other arithmetic: 17.6 us -> 0 us
    all_to_all x6 -> x0, waiting for transfers between devices: 224 us -> none  [the longest x2 175 us: on_device(): lax.all_to_all(potential_rows, 'row', split_axis=0, concat_axis=1, tiled=...]
    pallas_call x0 -> x3, Pallas kernels: none -> 188 us  [the longest x1 161 us: propagate(): pl.pallas_call(functools.partial(propagate_kernel, n, per), out_shape=jax...]
    all_to_all x6 -> x0, starting transfers between devices: 39.5 us -> none  [the longest x2 13.7 us: on_device(): lax.all_to_all(advanced, 'row', split_axis=1, concat_axis=0, tiled=True)]
    unnamed x15 -> x1, local copies, waits for them, and re-layouts: 32.4 us -> 0.97 us
    gather x12 -> x0, local copies, waits for them, and re-layouts: 22.3 us -> none  [the longest x2 15.2 us: on_device(): jnp.take(cholesky, slab_index[step_number], axis=0)]
    all_gather x1 -> x0, blocking collectives: 19 us -> none  [on_device(): all_fields = lax.all_gather(fields, 'row', axis=1, tiled=True)]
    dot_general x10 -> x0, matrix products: 18.8 us -> none  [the longest x8 9.39 us: taylor_step(): jnp.dot(potential, term_now, preferred_element_type=jnp.float32) / degree]
    select_n x9 -> x0, other arithmetic: 16 us -> none  [the longest x1 11.8 us: on_device(): jnp.take(cholesky, slab_index[step_number], axis=0)]
  transfers between devices with their start and end apart: 6 -> 0, of which waited for: 5 -> 0; matrix products, arithmetic and copies ran while one was open for 20% -> 0% of each run, Pallas kernels for 0% -> 0%
where the time goes in v1:
time: 190 us; the launch traced here: 189 us
  Pallas kernels  188 us (99%)
    pallas_call x1, Pallas kernels, propagate(): pl.pallas_call(functools.partial(propagate_kernel, n, per), out_shape=jax...  161 us
    pallas_call x1, Pallas kernels, make_potentials(): pl.pallas_call(functools.partial(potential_kernel, n, groups, per, block)...  18.3 us
    pallas_call x1, Pallas kernels, gather_fields(): pl.pallas_call(functools.partial(gather_kernel, n, groups), out_shape=(ja...  8.65 us

profile of v1, /device:TPU:9, one launch (start us, length us, event | category | flops | bytes accessed | tf_op | source)
XLA Modules:
  0.0 189.2 jit_solution(13450370486076227552)
XLA Ops:
  0.0 8.6 %gather_fields.1 = (f32[16,2,2,64]{3,2,1,0:T(2,128)}, s32[2,1,16]{2,1,0:T(1,128)}, s32[2,2,32]{2,1,0:T(2,128)}) custom-call(bf16[2,2,64]{2,1,0:T(2,128)(2,1)} %fields.1, s32[1,16]{1,0:T(1,128)} %bitcast.2, s32[2,32]{1,0:T(2,128)} %sources.1), custom_call_target="tpu_custom_call" | custom-call | tf_op jit(solution)/shard_map/gather_fields/pallas_call | solution.py:154
  8.7 18.3 %make_potentials.1 = (bf16[2,32,64,1024]{3,2,1,0:T(8,128)(2,1)}, bf16[32,64,256]{2,1,0:T(8,128)(2,1)S(1)}, s32[1,32]{1,0:T(1,128)S(1)}, s32[32]{0:T(128)S(1)}, s32[1]{0:T(128)}) custom-call(s32[2,64]{1,0:T(2,128)} %slab_index.1, s32[2,1,16]{2,1,0:T(1,128)} %get-tuple-element.40.counts, s32[2,2,32]{2,1,0:T(2,128)} %get-tuple-element.41.sources, ...), custom_call_target="tpu_custom_call" | custom-call | tf_op jit(solution)/shard_map/make_potentials/pallas_call | solution.py:333
  27.6 160.6 %conditional.1 = (bf16[32,64,256]{2,1,0:T(8,128)(2,1)S(1)}) conditional(s32[]{:T(128)} %bitcast.1, (bf16[2,32,64,1024]{3,2,1,0:T(8,128)(2,1)}, bf16[32,64,256]{2,1,0:T(8,128)(2,1)S(1)}, s32[1,32]{1,0:T(1,128)S(1)}, s32[32]{0:T(128)S(1)}) %tuple.11, (bf16[2,32,64,1024]{3,2,1,0:T(8,128)(2,1)}, bf16[32,64,256]{2,1,0:T(8,128)(2,1)S(1)}, ...), branch_computations={%region_0.0_spmd, %region_1.0_spmd} | conditional | bytes 8 | solution.py:555
  27.6 160.6 %propagate_1.1 = bf16[32,64,256]{2,1,0:T(8,128)(2,1)S(1)} custom-call(bf16[2,32,64,1024]{3,2,1,0:T(8,128)(2,1)} %get-tuple-element.28.potential, bf16[32,64,256]{2,1,0:T(8,128)(2,1)S(1)} %get-tuple-element.29.ordered, s32[1,32]{1,0:T(1,128)S(1)} %get-tuple-element.30.parents, s32[32]{0:T(128)S(1)} %get-tuple-element.31.picks), custom_call_target="tpu_custom_call" | custom-call | tf_op jit(solution)/shard_map/cond/branch_1_fun/propagate_1/pallas_call | solution.py:523
  188.2 1.0 copy.12

commit v2 on v1

--- a/solution.py
+++ b/solution.py
@@ -172,8 +172,33 @@
     )(fields, counts.reshape(1, n), sources)
 
 
+def room(n, share):
+    return sum(share[plane % 2] for plane in range(n // 4)) if share else n
+
+
+def seat(share, device):
+    if share is None:
+        return 1, device
+    plane, place = lax.div(device, 4), lax.rem(device, 4)
+    odd = lax.rem(plane, 2)
+    idle = 1 + 2 * lax.rem(lax.div(plane, 2) + plane, 2)
+    apart = place - idle
+
+    def of(taken):
+        if taken == 4:
+            return 1, place
+        if taken == 3:
+            return 1 - lax.div(9 - apart * apart, 9), place - lax.div(place + 3 - idle, 4)
+        return 1 - lax.rem(place, 2), lax.div(place, 2)
+
+    (even_busy, even_place), (odd_busy, odd_place) = of(share[0]), of(share[1])
+    first = lax.div(plane, 2) * (share[0] + share[1]) + odd * share[0]
+    busy = (1 - odd) * even_busy + odd * odd_busy
+    return busy, first + (1 - odd) * even_place + odd * odd_place
+
+
 def potential_kernel(
-    n, groups, per, block,
+    n, groups, per, block, shares,
     slab_index, counts, sources, fields, walkers, cholesky,
     potential, ordered, parents, picks, fits,
     chosen, made, left, spread, need, rank, slot, chol_sem, walk_sem, out_sem,
@@ -182,6 +207,7 @@
     slots = n * per
     rows, orbitals = chosen.shape[2], chosen.shape[3]
     group = lax.axis_index("groups")
+    unroll = slots <= 64
 
     def slab_copy(s, g):
         return pltpu.make_async_copy(
@@ -204,39 +230,39 @@
             return carry
 
         def live(j, carry):
-            need[steps, j] = (lax.rem(j, per) < counts[which, 0, j // per]).astype(jnp.int32)
-            return carry
-
-        lax.fori_loop(0, slots, clear, 0)
-        lax.fori_loop(0, slots, live, 0)
-        total = 0
+            need[steps, j] = (lax.rem(j, per) < counts[which, 0, lax.div(j, per)]).astype(jnp.int32)
+            return carry
+
+        lax.fori_loop(0, slots, clear, 0, unroll=unroll)
+        lax.fori_loop(0, slots, live, 0, unroll=unroll)
+        totals = [None] * steps
         for s in reversed(range(steps)):
             def mark(j, carry):
-                @pl.when(need[s + 1, j] == 1)
-                def _():
-                    need[s, sources[which, s, j]] = 1
-
+                picked = sources[which, s, j]
+                need[s, picked] = jnp.maximum(need[s, picked], need[s + 1, j])
                 return carry
 
             def number(j, count):
                 rank[s, j] = count
-
-                @pl.when(need[s, j] == 1)
-                def _():
-                    slot[s, count] = j
-
+                slot[s, count] = j
                 return count + need[s, j]
 
-            lax.fori_loop(0, slots, mark, 0)
-            count = lax.fori_loop(0, slots, number, jnp.int32(0))
-            total = jnp.maximum(total, count)
-        return total
-
-    largest = jnp.int32(0)
+            lax.fori_loop(0, slots, mark, 0, unroll=unroll)
+            totals[s] = lax.fori_loop(0, slots, number, jnp.int32(0), unroll=unroll)
+        return totals
+
+    most = [jnp.int32(0)] * steps
     for k in range(1, groups + 1):
         own = plan(lax.rem(group + k, groups))
-        largest = jnp.maximum(largest, own)
-    fits[0] = (largest <= n).astype(jnp.int32)
+        most = [jnp.maximum(a, b) for a, b in zip(most, own)]
+    largest = functools.reduce(jnp.maximum, most)
+    choice = jnp.int32(len(shares))
+    for place, share in reversed(list(enumerate(shares))):
+        enough = most[0] <= room(n, share[0])
+        for s in range(1, steps):
+            enough = jnp.logical_and(enough, most[s] <= room(n, share[s]))
+        choice = jnp.where(enough, place, choice)
+    fits[0] = choice
 
     def walker_copy(p):
         return pltpu.make_async_copy(walkers.at[slot[0, p]], ordered.at[p], walk_sem.at[p])
@@ -256,7 +282,7 @@
         picks[p] = alive * (1 + rank[steps - 1, sources[group, steps - 1, p]])
         return carry
 
-    lax.fori_loop(0, slots, parent, 0)
+    lax.fori_loop(0, slots, parent, 0, unroll=unroll)
 
     wide = slab * block
     column = lax.broadcasted_iota(jnp.int32, (slab, wide), 1)
@@ -269,13 +295,13 @@
     def build(s, q):
         def field_row(p, carry):
             index = slot[s, q * n + p]
-            line = fields[index // per, s, pl.ds(lax.rem(index, per), 1), :]
+            line = fields[lax.div(index, per), s, pl.ds(lax.rem(index, per), 1), :]
             spread[pl.ds(pl.multiple_of(p * block, block), block), :] = jnp.broadcast_to(
                 line, (block, slab)
             )
             return carry
 
-        lax.fori_loop(0, n, field_row, 0)
+        lax.fori_loop(0, n, field_row, 0, unroll=unroll)
         across = jnp.dot(
             spread[...].astype(jnp.bfloat16), expand, preferred_element_type=jnp.float32
         )
@@ -322,7 +348,7 @@
     lax.fori_loop(0, slots, walker_here, 0)
 
 
-def make_potentials(n, groups, slab_index, counts, sources, fields, walkers, cholesky):
+def make_potentials(n, groups, shares, slab_index, counts, sources, fields, walkers, cholesky):
     _, steps, per, slab = fields.shape
     slots, rows, electrons = walkers.shape
     orbitals = cholesky.shape[2]
@@ -331,7 +357,7 @@
     vmem = pl.BlockSpec(memory_space=pltpu.VMEM)
     anywhere = pl.BlockSpec(memory_space=pl.ANY)
     return pl.pallas_call(
-        functools.partial(potential_kernel, n, groups, per, block),
+        functools.partial(potential_kernel, n, groups, per, block, shares),
         out_shape=(
             jax.ShapeDtypeStruct((steps, slots, rows, orbitals), jnp.bfloat16),
             jax.ShapeDtypeStruct((slots, rows, electrons), jnp.bfloat16),
@@ -359,7 +385,7 @@
 
 
 def propagate_kernel(
-    n, per, potential, ordered, parents, picks, out,
+    n, per, share, potential, ordered, parents, picks, out,
     matrices, columns, term, summed, advanced, turned, back0, back1,
     v_send, v_recv, w_send, w_recv, r_send, r_recv, own_sem,
 ):
@@ -368,6 +394,7 @@
     electrons = ordered.shape[2]
     me = lax.axis_index("row")
     back = (back0, back1)
+    place = [seat(share[s], me)[1] for s in range(steps)]
 
     def copy(source, target, sends, recvs, k):
         return pltpu.make_async_remote_copy(
@@ -381,7 +408,7 @@
 
     def v_copy(s, q, k, owner):
         return copy(
-            potential.at[s, q * n + lax.rem(me + k, n)],
+            potential.at[s, q * n + seat(share[s], lax.rem(me + k, n))[1]],
             matrices.at[s, q, owner],
             v_send.at[s, q, k],
             v_recv.at[s, q, k],
@@ -391,7 +418,7 @@
     def w_copy(s, q, k, owner):
         source = ordered if s == 0 else turned
         return copy(
-            source.at[q * n + lax.rem(me + k, n)],
+            source.at[q * n + seat(share[s], lax.rem(me + k, n))[1]],
             columns.at[s, q, owner],
             w_send.at[s, q, k],
             w_recv.at[s, q, k],
@@ -401,7 +428,7 @@
     def r_copy(s, q, k, owner):
         return copy(
             advanced.at[s, q, lax.rem(me + k, n)],
-            back[s].at[1 + q * n + owner],
+            back[s].at[1 + q * n + seat(share[s], owner)[1]],
             r_send.at[s, q, k],
             r_recv.at[s, q, k],
             k,
@@ -409,37 +436,42 @@
 
     def own_v(s, q):
         return pltpu.make_async_copy(
-            potential.at[s, q * n + me], matrices.at[s, q, me], own_sem.at[s, q]
+            potential.at[s, q * n + place[s]], matrices.at[s, q, me], own_sem.at[s, q]
         )
 
     def own_w(q):
         return pltpu.make_async_copy(
-            ordered.at[q * n + me], columns.at[0, q, me], own_sem.at[steps, q]
-        )
+            ordered.at[q * n + place[0]], columns.at[0, q, me], own_sem.at[steps, q]
+        )
+
+    def when(s, device):
+        return pl.when(seat(share[s], device)[0] == 1) if share[s] else lambda body: body()
+
+    def over(s, owned, turn, first=1, last=n):
+        def one(k, carry):
+            other = lax.rem(me + owned * k + n, n)
+
+            @when(s, other if owned else me)
+            def _():
+                for q in range(per):
+                    turn(q, k)
+
+            return carry
+
+        lax.fori_loop(first, last, one, 0)
 
     def start(make, s, first=1, last=n):
-        def one(k, carry):
-            for q in range(per):
-                make(s, q, k, me).start()
-            return carry
-
-        lax.fori_loop(first, last, one, 0)
+        over(s, 0 if make is r_copy else 1, lambda q, k: make(s, q, k, me).start(), first, last)
 
     def received(make, s):
-        def one(k, carry):
-            for q in range(per):
-                make(s, q, k, lax.rem(me - k + n, n)).wait_recv()
-            return carry
-
-        lax.fori_loop(1, n, one, 0)
+        over(
+            s,
+            -1 if make is r_copy else 0,
+            lambda q, k: make(s, q, k, lax.rem(me - k + n, n)).wait_recv(),
+        )
 
     def sent(make, s):
-        def one(k, carry):
-            for q in range(per):
-                make(s, q, k, me).wait_send()
-            return carry
-
-        lax.fori_loop(1, n, one, 0)
+        over(s, 0 if make is r_copy else 1, lambda q, k: make(s, q, k, me).wait_send())
 
     def taylor(s, q):
         term[0] = columns[s, q].reshape(n * rows, electrons)
@@ -465,40 +497,69 @@
         advanced[s, q] = summed[...].astype(jnp.bfloat16).reshape(n, rows, electrons)
 
     for s in range(steps):
-        back[s][0] = jnp.zeros((rows, electrons), jnp.bfloat16)
+        for p in [0] + list(range(1 + per * room(n, share[s]), 1 + per * n)):
+            back[s][p] = jnp.zeros((rows, electrons), jnp.bfloat16)
     enter(n, 1, me, 0, False)
     start(w_copy, 0)
     start(v_copy, 0)
-    for q in range(per):
-        own_w(q).start()
-        for s in range(steps):
-            own_v(s, q).start()
-    for q in range(per):
-        own_w(q).wait()
-        for s in range(steps):
-            own_v(s, q).wait()
+    @when(0, me)
+    def _():
+        for q in range(per):
+            own_w(q).start()
+            own_v(0, q).start()
+
+    for s in range(1, steps):
+        @when(s, me)
+        def _():
+            for q in range(per):
+                own_v(s, q).start()
+
+    @when(0, me)
+    def _():
+        for q in range(per):
+            own_w(q).wait()
+            own_v(0, q).wait()
+
+    for s in range(1, steps):
+        @when(s, me)
+        def _():
+            for q in range(per):
+                own_v(s, q).wait()
+
     received(w_copy, 0)
     received(v_copy, 0)
     for s in range(steps):
         if s + 1 < steps:
             start(v_copy, s + 1, 1, n // 2)
-        for q in range(per):
-            taylor(s, q)
+
+        @when(s, me)
+        def _():
+            for q in range(per):
+                taylor(s, q)
+
         start(r_copy, s)
         if s + 1 < steps:
             start(v_copy, s + 1, n // 2, n)
-        for q in range(per):
-            back[s][1 + q * n + me] = advanced[s, q, me]
+
+        @when(s, me)
+        def _():
+            for q in range(per):
+                back[s][1 + q * n + place[s]] = advanced[s, q, me]
+
         received(r_copy, s)
         if s + 1 < steps:
             def turn(p, carry):
                 turned[p] = back[s][parents[s, p]]
                 return carry
 
-            lax.fori_loop(0, n * per, turn, 0)
+            lax.fori_loop(0, per * room(n, share[s + 1]), turn, 0)
             start(w_copy, s + 1)
-            for q in range(per):
-                columns[s + 1, q, me] = turned[q * n + me]
+
+            @when(s + 1, me)
+            def _():
+                for q in range(per):
+                    columns[s + 1, q, me] = turned[q * n + place[s + 1]]
+
             received(w_copy, s + 1)
             received(v_copy, s + 1)
 
@@ -512,7 +573,7 @@
             sent(make, s)
 
 
-def propagate(n, per, ident, potential, ordered, parents, picks):
+def propagate(n, per, share, ident, potential, ordered, parents, picks):
     steps, slots, rows, orbitals = potential.shape
     electrons = ordered.shape[2]
     smem = pl.BlockSpec(memory_space=pltpu.SMEM)
@@ -521,7 +582,7 @@
     half = jnp.bfloat16
     pairs = pltpu.SemaphoreType.DMA((steps, per, n))
     return pl.pallas_call(
-        functools.partial(propagate_kernel, n, per),
+        functools.partial(propagate_kernel, n, per, share),
         out_shape=jax.ShapeDtypeStruct((slots, rows, electrons), half),
         in_specs=[anywhere, anywhere, smem, smem],
         out_specs=vmem,
@@ -540,24 +601,24 @@
         compiler_params=pltpu.CompilerParams(
             collective_id=ident, has_side_effects=True, vmem_limit_bytes=VMEM_BYTES
         ),
-        name="propagate_%d" % per,
+        name="propagate_%d" % ident,
     )(potential, ordered, parents, picks)
 
 
 def on_device(n, groups, walkers, cholesky, slab_index, fields, counts, sources):
     if walkers.shape[1] % 16:
         return thin_rows(walkers, cholesky, slab_index, fields, counts, sources)
-    per = fields.shape[1]
+    steps, per = fields.shape[:2]
+    shares = [(None,) * steps]
+    if n % 4 == 0 and steps == 2:
+        shares = [((3, 2), (3, 3)), ((3, 3), (4, 3))] + shares
     all_fields, all_counts, all_sources = gather_fields(n, groups, fields, counts, sources)
     potential, ordered, parents, picks, fits = make_potentials(
-        n, groups, slab_index, all_counts, all_sources, all_fields, walkers, cholesky
+        n, groups, shares, slab_index, all_counts, all_sources, all_fields, walkers, cholesky
     )
-    return lax.cond(
-        fits[0] == 1,
-        lambda *args: propagate(n, 1, 1, *args),
-        lambda *args: propagate(n, per, 2, *args),
-        potential, ordered, parents, picks,
-    )
+    branches = [functools.partial(propagate, n, 1, share, 1 + i) for i, share in enumerate(shares)]
+    branches.append(functools.partial(propagate, n, per, (None,) * steps, 1 + len(shares)))
+    return lax.switch(fits[0], branches, potential, ordered, parents, picks)
 
 
 def solution(mesh):

time: 190 us -> 143 us (0.75)
  Pallas kernels: 188 us -> 139 us
    pallas_call x2, Pallas kernels: 179 us -> 131 us  [the longest x1 114 us: propagate(): pl.pallas_call(functools.partial(propagate_kernel, n, per, share), out_sh...]
where the time goes in v2:
time: 143 us; the launch traced here: 141 us
  Pallas kernels  139 us (97%)
    pallas_call x1, Pallas kernels, propagate(): pl.pallas_call(functools.partial(propagate_kernel, n, per, share), out_sh...  114 us
    pallas_call x1, Pallas kernels, make_potentials(): pl.pallas_call(functools.partial(potential_kernel, n, groups, per, block,...  16.2 us
    pallas_call x1, Pallas kernels, gather_fields(): pl.pallas_call(functools.partial(gather_kernel, n, groups), out_shape=(ja...  8.65 us

profile of v2, /device:TPU:9, one launch (start us, length us, event | category | flops | bytes accessed | tf_op | source)
XLA Modules:
  0.0 141.2 jit_solution(1172632900041316891)
XLA Ops:
  0.0 8.6 %gather_fields.1 = (f32[16,2,2,64]{3,2,1,0:T(2,128)}, s32[2,1,16]{2,1,0:T(1,128)}, s32[2,2,32]{2,1,0:T(2,128)}) custom-call(bf16[2,2,64]{2,1,0:T(2,128)(2,1)} %fields.1, s32[1,16]{1,0:T(1,128)} %bitcast.2, s32[2,32]{1,0:T(2,128)} %sources.1), custom_call_target="tpu_custom_call" | custom-call | tf_op jit(solution)/shard_map/gather_fields/pallas_call | solution.py:154
  8.7 16.2 %make_potentials.1 = (bf16[2,32,64,1024]{3,2,1,0:T(8,128)(2,1)}, bf16[32,64,256]{2,1,0:T(8,128)(2,1)S(1)}, s32[1,32]{1,0:T(1,128)S(1)}, s32[32]{0:T(128)S(1)}, s32[1]{0:T(128)}) custom-call(s32[2,64]{1,0:T(2,128)} %slab_index.1, s32[2,1,16]{2,1,0:T(1,128)} %get-tuple-element.66.counts, s32[2,2,32]{2,1,0:T(2,128)} %get-tuple-element.67.sources, ...), custom_call_target="tpu_custom_call" | custom-call | tf_op jit(solution)/shard_map/make_potentials/pallas_call | solution.py:359
  25.5 114.7 %conditional.1 = (bf16[32,64,256]{2,1,0:T(8,128)(2,1)S(1)}) conditional(s32[]{:T(128)} %bitcast.1, (bf16[2,32,64,1024]{3,2,1,0:T(8,128)(2,1)}, bf16[32,64,256]{2,1,0:T(8,128)(2,1)S(1)}, s32[1,32]{1,0:T(1,128)S(1)}, s32[32]{0:T(128)S(1)}) %tuple.17, (bf16[2,32,64,1024]{3,2,1,0:T(8,128)(2,1)}, ...), branch_computations={%region_0.0_spmd, %region_1.0_spmd, %region_2.0_spmd, %region_3.0_... | conditional | bytes 8 | solution.py:621
  25.5 114.5 %propagate_1.1 = bf16[32,64,256]{2,1,0:T(8,128)(2,1)S(1)} custom-call(bf16[2,32,64,1024]{3,2,1,0:T(8,128)(2,1)} %get-tuple-element.40.potential, bf16[32,64,256]{2,1,0:T(8,128)(2,1)S(1)} %get-tuple-element.42.ordered, s32[1,32]{1,0:T(1,128)S(1)} %get-tuple-element.44.parents, s32[32]{0:T(128)S(1)} %get-tuple-element.45.picks), custom_call_target="tpu_custom_call" | custom-call | tf_op jit(solution)/shard_map/cond/branch_0_fun/propagate_1/pallas_call | solution.py:584
  140.2 1.0 copy.16
